TPU v7x, 32 devices: a whole 2x2x4 slice. The times are simulated.
32 devices in a mesh: groups: 2 (over x), col: 16 (over z, y, core).
Axes of the slice: x: 2, y: 2, z: 4, core: 2. Of those that a mesh axis runs over, the one named last changes fastest.
Arguments:
- left: bfloat16 [256, 64, 32], P('col', 'groups'), parts along dimension 1, may hold values from -18 to 18
- right: bfloat16 [256, 2560, 32], P('col', 'groups'), parts along dimension 1, may hold values from -18 to 18
- out_weight: bfloat16 [1024, 128], replicated, may hold values from -0.1875 to 0.1875
- out_bias: float32 [128], replicated, may hold values from -3 to 3
Outputs:
- pair_update: bfloat16 [64, 1280, 128], P('groups', 'col'), parts along dimension 0
There are 2 independent parts, one for each index of `groups`. A program takes and returns all parts, laid end to end along the dimension named above; an argument that names none is the same for every part. Nothing has to cross between parts.
All inputs are finite; a program needn't handle non-finite values.
Results may differ from a plain program's by a relative error of at most 0.004.
Values may be sent and summed in bfloat16 or wider, within the bound.
A program may use at most 64 MiB of HBM per device.

v0:
```python
import jax
import jax.numpy as jnp
from jax import lax
from jax.sharding import PartitionSpec as P


def tile_update(left_rows, right_cols, out_weight, out_bias):
    seqs, count, width = left_rows.shape
    columns = right_cols.shape[1]
    outer = (
        jnp.einsum("sic,sje->ijce", left_rows, right_cols, preferred_element_type=jnp.float32)
        / seqs
    )
    flat = outer.astype(jnp.bfloat16).reshape(count * columns, width * width)
    update = jnp.dot(flat, out_weight, preferred_element_type=jnp.float32) + out_bias
    return update.astype(jnp.bfloat16).reshape(count, columns, out_weight.shape[1])


def rows_update(left_rows, right_cols, out_weight, out_bias):
    seqs, count, width = left_rows.shape
    blocks = jnp.transpose(left_rows.reshape(seqs, count // 8, 8, width), (1, 0, 2, 3))
    results = lax.map(lambda block: tile_update(block, right_cols, out_weight, out_bias), blocks)
    return results.reshape(count, right_cols.shape[1], out_weight.shape[1])


def on_device(left, right, out_weight, out_bias):
    left_part, right_cols = (
        lax.all_to_all(left, "col", split_axis=1, concat_axis=0, tiled=True),
        lax.all_to_all(right, "col", split_axis=1, concat_axis=0, tiled=True),
    )
    return rows_update(
        lax.all_gather(left_part, "col", axis=1, tiled=True), right_cols, out_weight, out_bias
    )


def solution(mesh):
    in_specs = (P("col", "groups", None), P("col", "groups", None), P(), P())
    out_specs = P("groups", "col", None)
    return jax.shard_map(
        on_device, mesh=mesh, in_specs=in_specs, out_specs=out_specs, check_vma=False
    )
```

profile of v0, /device:TPU:9, one launch (start us, length us, event | category | flops | bytes accessed | tf_op | source)
XLA Modules:
  0.0 118.3 jit_solution(4670310625103489706)
XLA Ops:
  0.0 1.0 copy.21
  1.0 0.8 reshape.16
  1.7 6.6 %all-to-all-start = ((bf16[16,2,512]{2,1,0:T(2,128)(2,1)}), bf16[16,2,512]{2,1,0:T(2,128)(2,1)S(1)}, u32[]{:S(2)}, u32[]{:S(2)}) async-start(bf16[16,2,512]{2,1,0:T(2,128)(2,1)} %reshape.16), calls=%async_computation | async-start | bytes 65536 | tf_op jit(solution)/shard_map/all_to_all | solution.py:28
  8.3 6.9 %copy.16 = bf16[16,1280,32]{2,0,1:T(8,128)(2,1)} copy(bf16[16,1280,32]{1,2,0:T(8,128)(2,1)} %param.7) | data formatting | bytes 2621440 | tf_op args[1]
  15.2 8.3 %reshape.18 = bf16[16,2,20480]{2,1,0:T(2,128)(2,1)} reshape(bf16[1280,16,32]{2,1,0:T(8,128)(2,1)} %bitcast.49) | data formatting | bytes 2621440
  23.5 0.0 all-to-all-done
  23.5 6.0 %all-to-all-start.1 = ((bf16[16,2,20480]{2,1,0:T(2,128)(2,1)}), bf16[16,2,20480]{2,1,0:T(2,128)(2,1)S(1)}, u32[]{:S(2)}, u32[]{:S(2)}) async-start(bf16[16,2,20480]{2,1,0:T(2,128)(2,1)} %reshape.18), calls=%async_computation.1 | async-start | bytes 2621440 | tf_op jit(solution)/shard_map/all_to_all | solution.py:29
  29.5 0.1 reshape.17
  29.7 0.1 copy.15
  29.8 43.8 %all_gather.3 = bf16[256,32,32]{0,2,1:T(8,128)(2,1)} all-gather(bf16[256,2,32]{0,2,1:T(8,128)(2,1)S(1)} %copy.15), channel_id=1, replica_groups=mesh['groups'=2,'col'=16] {'col'}, dimensions={1}, use_global_device_ids=true | all-gather | bytes 557056 | tf_op jit(solution)/shard_map/all_gather | solution.py:32
  73.6 0.0 all-to-all-done.1
  73.6 4.0 %reshape.19 = bf16[1280,16,32]{2,1,0:T(8,128)(2,1)} reshape(bf16[16,2,20480]{2,1,0:T(2,128)(2,1)S(1)} %all-to-all-done.1) | data formatting | bytes 2621440
  77.6 6.8 %copy.17 = bf16[16,16,80,32]{2,3,0,1:T(8,128)(2,1)S(1)} copy(bf16[16,16,80,32]{3,0,2,1:T(8,128)(2,1)} %bitcast.48) | data formatting | bytes 2621440 | tf_op jit(solution)/shard_map/all_to_all | solution.py:29
  84.4 0.0 copy-start.2
  84.4 1.6 %copy.18 = bf16[256,80,32]{0,1,2:T(8,128)(2,1)S(1)} copy(bf16[256,80,32]{1,2,0:T(8,128)(2,1)S(1)} %bitcast.51) | data formatting | bytes 2621440 | tf_op jit(solution)/shard_map/while | solution.py:22
  86.0 0.0 copy-done.2
  86.0 32.3 %while.10 = (s32[]{:T(128)}, bf16[4,8,80,128]{3,2,1,0:T(8,128)(2,1)}, bf16[4,256,8,32]{1,3,2,0:T(8,128)(2,1)}, bf16[256,80,32]{0,1,2:T(8,128)(2,1)S(1)}, bf16[10...) while((s32[]{:T(128)}, bf16[4,8,80,128]{3,2,1,0:T(8,128)(2,1)}, bf16[4,256,8,32]{1,3,2,0:T(8,128)(2,1)}, ...), condition=%wide.region_1.2_spmd, body=%wide.region_0.1_spmd.sunk | while | flops 504791040 | bytes 20547204 | solution.py:22
  86.0 0.0 copy-start
  86.0 1.1 copy-done
  87.1 1.6 %fusion.18 = bf16[8,80,32,32]{1,2,3,0:T(8,128)(2,1)S(1)} fusion(bf16[256,80,32]{0,1,2:T(8,128)(2,1)S(1)} %get-tuple-element.116, bf16[4,256,8,32]{1,3,2,0:T(8,128)(2,1)} %get-tuple-element.115, s32[]{:T(128)} %get-tuple-element.106), kind=kOutput, calls=%fused_computation.1.clone.1 | convolution fusion | flops 336855040 | bytes 2753024 | tf_op jit(solution)/shard_map/while/body/eval_jaxpr/sic,sje->ijce/dot_general | solution.py:11
  88.7 1.4 %copy.23 = bf16[8,80,32,32]{1,0,3,2:T(8,128)(2,1)S(1)} copy(bf16[8,80,32,32]{1,2,3,0:T(8,128)(2,1)S(1)} %fusion.18) | data formatting | bytes 2621440 | tf_op jit(solution)/shard_map/while/body/eval_jaxpr/convert_element_type | solution.py:14
  90.1 1.7 %reshape.21 = bf16[640,1024]{0,1:T(8,128)(2,1)S(1)} reshape(bf16[8,80,32,32]{1,0,3,2:T(8,128)(2,1)S(1)} %copy.23) | data formatting | bytes 2621440 | tf_op jit(solution)/shard_map/while/body/eval_jaxpr/reshape | solution.py:14
  91.8 0.0 copy-start.1
  91.8 1.6 %fusion.19 = bf16[640,128]{1,0:T(8,128)(2,1)S(1)} fusion(bf16[640,1024]{0,1:T(8,128)(2,1)S(1)} %reshape.21, bf16[1024,128]{1,0:T(8,128)(2,1)} %get-tuple-element.117, f32[128]{0:T(128)S(1)} %get-tuple-element.118), kind=kOutput, calls=%fused_computation.4.clone.1 | convolution fusion | flops 167936000 | bytes 1737216 | tf_op jit(solution)/shard_map/while/body/eval_jaxpr/dot_general | solution.py:15
  93.4 0.7 constant_dynamic-update-slice_fusion.2
  94.1 0.0 copy-done.1
  94.1 1.1 copy-done
  95.2 1.6 %fusion.18 = bf16[8,80,32,32]{1,2,3,0:T(8,128)(2,1)S(1)} fusion(bf16[256,80,32]{0,1,2:T(8,128)(2,1)S(1)} %get-tuple-element.116, bf16[4,256,8,32]{1,3,2,0:T(8,128)(2,1)} %get-tuple-element.115, s32[]{:T(128)} %get-tuple-element.106), kind=kOutput, calls=%fused_computation.1.clone.1 | convolution fusion | flops 336855040 | bytes 2753024 | tf_op jit(solution)/shard_map/while/body/eval_jaxpr/sic,sje->ijce/dot_general | solution.py:11
  96.8 1.4 %copy.23 = bf16[8,80,32,32]{1,0,3,2:T(8,128)(2,1)S(1)} copy(bf16[8,80,32,32]{1,2,3,0:T(8,128)(2,1)S(1)} %fusion.18) | data formatting | bytes 2621440 | tf_op jit(solution)/shard_map/while/body/eval_jaxpr/convert_element_type | solution.py:14
  98.2 1.7 %reshape.21 = bf16[640,1024]{0,1:T(8,128)(2,1)S(1)} reshape(bf16[8,80,32,32]{1,0,3,2:T(8,128)(2,1)S(1)} %copy.23) | data formatting | bytes 2621440 | tf_op jit(solution)/shard_map/while/body/eval_jaxpr/reshape | solution.py:14
  99.9 0.0 copy-start.1
  99.9 1.6 %fusion.19 = bf16[640,128]{1,0:T(8,128)(2,1)S(1)} fusion(bf16[640,1024]{0,1:T(8,128)(2,1)S(1)} %reshape.21, bf16[1024,128]{1,0:T(8,128)(2,1)} %get-tuple-element.117, f32[128]{0:T(128)S(1)} %get-tuple-element.118), kind=kOutput, calls=%fused_computation.4.clone.1 | convolution fusion | flops 167936000 | bytes 1737216 | tf_op jit(solution)/shard_map/while/body/eval_jaxpr/dot_general | solution.py:15
  101.5 0.7 constant_dynamic-update-slice_fusion.2
  102.2 0.0 copy-done.1
  102.2 1.1 copy-done
  103.2 1.6 %fusion.18 = bf16[8,80,32,32]{1,2,3,0:T(8,128)(2,1)S(1)} fusion(bf16[256,80,32]{0,1,2:T(8,128)(2,1)S(1)} %get-tuple-element.116, bf16[4,256,8,32]{1,3,2,0:T(8,128)(2,1)} %get-tuple-element.115, s32[]{:T(128)} %get-tuple-element.106), kind=kOutput, calls=%fused_computation.1.clone.1 | convolution fusion | flops 336855040 | bytes 2753024 | tf_op jit(solution)/shard_map/while/body/eval_jaxpr/sic,sje->ijce/dot_general | solution.py:11
  104.9 1.4 %copy.23 = bf16[8,80,32,32]{1,0,3,2:T(8,128)(2,1)S(1)} copy(bf16[8,80,32,32]{1,2,3,0:T(8,128)(2,1)S(1)} %fusion.18) | data formatting | bytes 2621440 | tf_op jit(solution)/shard_map/while/body/eval_jaxpr/convert_element_type | solution.py:14
  106.2 1.7 %reshape.21 = bf16[640,1024]{0,1:T(8,128)(2,1)S(1)} reshape(bf16[8,80,32,32]{1,0,3,2:T(8,128)(2,1)S(1)} %copy.23) | data formatting | bytes 2621440 | tf_op jit(solution)/shard_map/while/body/eval_jaxpr/reshape | solution.py:14
  107.9 0.0 copy-start.1
  108.0 1.6 %fusion.19 = bf16[640,128]{1,0:T(8,128)(2,1)S(1)} fusion(bf16[640,1024]{0,1:T(8,128)(2,1)S(1)} %reshape.21, bf16[1024,128]{1,0:T(8,128)(2,1)} %get-tuple-element.117, f32[128]{0:T(128)S(1)} %get-tuple-element.118), kind=kOutput, calls=%fused_computation.4.clone.1 | convolution fusion | flops 167936000 | bytes 1737216 | tf_op jit(solution)/shard_map/while/body/eval_jaxpr/dot_general | solution.py:15
  109.6 0.7 constant_dynamic-update-slice_fusion.2
  110.2 0.0 copy-done.1
  110.2 1.1 copy-done
  111.3 1.6 %fusion.18 = bf16[8,80,32,32]{1,2,3,0:T(8,128)(2,1)S(1)} fusion(bf16[256,80,32]{0,1,2:T(8,128)(2,1)S(1)} %get-tuple-element.116, bf16[4,256,8,32]{1,3,2,0:T(8,128)(2,1)} %get-tuple-element.115, s32[]{:T(128)} %get-tuple-element.106), kind=kOutput, calls=%fused_computation.1.clone.1 | convolution fusion | flops 336855040 | bytes 2753024 | tf_op jit(solution)/shard_map/while/body/eval_jaxpr/sic,sje->ijce/dot_general | solution.py:11
  113.0 1.4 %copy.23 = bf16[8,80,32,32]{1,0,3,2:T(8,128)(2,1)S(1)} copy(bf16[8,80,32,32]{1,2,3,0:T(8,128)(2,1)S(1)} %fusion.18) | data formatting | bytes 2621440 | tf_op jit(solution)/shard_map/while/body/eval_jaxpr/convert_element_type | solution.py:14
  114.3 1.7 %reshape.21 = bf16[640,1024]{0,1:T(8,128)(2,1)S(1)} reshape(bf16[8,80,32,32]{1,0,3,2:T(8,128)(2,1)S(1)} %copy.23) | data formatting | bytes 2621440 | tf_op jit(solution)/shard_map/while/body/eval_jaxpr/reshape | solution.py:14
  116.0 1.6 %fusion.19 = bf16[640,128]{1,0:T(8,128)(2,1)S(1)} fusion(bf16[640,1024]{0,1:T(8,128)(2,1)S(1)} %reshape.21, bf16[1024,128]{1,0:T(8,128)(2,1)} %get-tuple-element.117, f32[128]{0:T(128)S(1)} %get-tuple-element.118), kind=kOutput, calls=%fused_computation.4.clone.1 | convolution fusion | flops 167936000 | bytes 1737216 | tf_op jit(solution)/shard_map/while/body/eval_jaxpr/dot_general | solution.py:15
  117.6 0.7 constant_dynamic-update-slice_fusion.2
  (7 shorter events, 0.0 us)
Async XLA Ops:
  1.7 21.8 %all-to-all-start = ((bf16[16,2,512]{2,1,0:T(2,128)(2,1)}), bf16[16,2,512]{2,1,0:T(2,128)(2,1)S(1)}, u32[]{:S(2)}, u32[]{:S(2)}) async-start(bf16[16,2,512]{2,1,0:T(2,128)(2,1)} %reshape.16), calls=%async_computation | async-start | bytes 65536 | tf_op jit(solution)/shard_map/all_to_all | solution.py:28
  23.5 50.1 %all-to-all-start.1 = ((bf16[16,2,20480]{2,1,0:T(2,128)(2,1)}), bf16[16,2,20480]{2,1,0:T(2,128)(2,1)S(1)}, u32[]{:S(2)}, u32[]{:S(2)}) async-start(bf16[16,2,20480]{2,1,0:T(2,128)(2,1)} %reshape.18), calls=%async_computation.1 | async-start | bytes 2621440 | tf_op jit(solution)/shard_map/all_to_all | solution.py:29
  84.4 1.6 %copy-start.2 = (f32[128]{0:T(128)S(1)}, f32[128]{0:T(128)}, u32[]{:S(2)}) copy-start(f32[128]{0:T(128)} %param.9) | copy-start | bytes 1540
  86.0 1.1 copy-start
  91.8 2.3 %copy-start.1 = (bf16[256,80,32]{0,1,2:T(8,128)(2,1)S(1)}, bf16[256,80,32]{0,1,2:T(8,128)(2,1)}, u32[]{:S(2)}) copy-start(bf16[256,80,32]{0,1,2:T(8,128)(2,1)} %copy-done) | copy-start | bytes 3932164 | tf_op jit(solution)/shard_map/while
  94.1 1.1 copy-start
  99.9 2.3 %copy-start.1 = (bf16[256,80,32]{0,1,2:T(8,128)(2,1)S(1)}, bf16[256,80,32]{0,1,2:T(8,128)(2,1)}, u32[]{:S(2)}) copy-start(bf16[256,80,32]{0,1,2:T(8,128)(2,1)} %copy-done) | copy-start | bytes 3932164 | tf_op jit(solution)/shard_map/while
  102.2 1.1 copy-start
  107.9 2.3 %copy-start.1 = (bf16[256,80,32]{0,1,2:T(8,128)(2,1)S(1)}, bf16[256,80,32]{0,1,2:T(8,128)(2,1)}, u32[]{:S(2)}) copy-start(bf16[256,80,32]{0,1,2:T(8,128)(2,1)} %copy-done) | copy-start | bytes 3932164 | tf_op jit(solution)/shard_map/while
  110.2 1.1 copy-start
  116.0 2.3 %copy-start.1 = (bf16[256,80,32]{0,1,2:T(8,128)(2,1)S(1)}, bf16[256,80,32]{0,1,2:T(8,128)(2,1)}, u32[]{:S(2)}) copy-start(bf16[256,80,32]{0,1,2:T(8,128)(2,1)} %copy-done) | copy-start | bytes 3932164 | tf_op jit(solution)/shard_map/while
where the time goes:
time: 119 us; the launch traced here: 118 us
  local copies, waits for them, and re-layouts  48.7 us (41%)
  blocking collectives  43.8 us (37%)
  matrix products  12.9 us (11%)
  starting transfers between devices  12.6 us (11%)
    all_gather x1, blocking collectives, on_device(): lax.all_gather(left_part, 'col', axis=1, tiled=True)  43.8 us
    unnamed x8, local copies, waits for them, and re-layouts  21.1 us
    reshape x4, local copies, waits for them, and re-layouts, tile_update(): flat = outer.astype(jnp.bfloat16).reshape(count * columns, width * width)  6.79 us
    all_to_all x1, local copies, waits for them, and re-layouts, on_device(): lax.all_to_all(right, 'col', split_axis=1, concat_axis=0, tiled=True)  6.76 us
    all_to_all x1, starting transfers between devices, on_device(): lax.all_to_all(left, 'col', split_axis=1, concat_axis=0, tiled=True)  6.58 us
    dot_general x4, matrix products, tile_update(): jnp.einsum('sic,sje->ijce', left_rows, right_cols, preferred_element_type...  6.53 us
    dot_general x4, matrix products, tile_update(): jnp.dot(flat, out_weight, preferred_element_type=jnp.float32) + out_bias  6.39 us
    all_to_all x1, starting transfers between devices, on_device(): lax.all_to_all(right, 'col', split_axis=1, concat_axis=0, tiled=True)  6.02 us
  transfers between devices with their start and end apart: 2, of which 0 were waited for; matrix products, arithmetic and copies ran while one was open for 13% of the time, Pallas kernels for 0%

commit v1 on v0

--- a/solution.py
+++ b/solution.py
@@ -1,7 +1,23 @@
+import functools
 import jax
 import jax.numpy as jnp
 from jax import lax
 from jax.sharding import PartitionSpec as P
+
+
+def _resolve_series_all(x_local, peer_axis):
+    tall, arr_next = (jax.lax.axis_size(peer_axis), jax.lax.axis_index(peer_axis))
+    taken_in, y = (x_local, 1)
+    while y < tall:
+        item_now = jax.lax.ppermute(taken_in, peer_axis, [(j0, j0 ^ y) for j0 in range(tall)])
+        state_next = jnp.concatenate([taken_in, item_now], axis=1)
+        later = jnp.concatenate([item_now, taken_in], axis=1)
+        taken_in = jnp.where(arr_next & y == 0, state_next, later)
+        y = 2 * y
+    return taken_in
+
+
+search_the_ticks = functools.partial(_resolve_series_all, peer_axis="col")
 
 
 def tile_update(left_rows, right_cols, out_weight, out_bias):
@@ -28,9 +44,7 @@
         lax.all_to_all(left, "col", split_axis=1, concat_axis=0, tiled=True),
         lax.all_to_all(right, "col", split_axis=1, concat_axis=0, tiled=True),
     )
-    return rows_update(
-        lax.all_gather(left_part, "col", axis=1, tiled=True), right_cols, out_weight, out_bias
-    )
+    return rows_update(search_the_ticks(left_part), right_cols, out_weight, out_bias)
 
 
 def solution(mesh):

time: 119 us -> 120 us (level)
  the two profiles are of different devices: /device:TPU:9 before, /device:TPU:0 now
where the time goes in v1:
time: 120 us; the launch traced here: 119 us
  local copies, waits for them, and re-layouts  48.9 us (41%)
  waiting for transfers between devices  36.1 us (30%)
  starting transfers between devices  20.3 us (17%)
  matrix products  12.9 us (11%)
    ppermute x4, waiting for transfers between devices, _resolve_series_all(): jax.lax.ppermute(taken_in, peer_axis, [(j0, j0 ^ y) for j0 in range(tall)])  36.1 us
    unnamed x8, local copies, waits for them, and re-layouts  21.1 us
    all_to_all x1, starting transfers between devices, on_device(): lax.all_to_all(left, 'col', split_axis=1, concat_axis=0, tiled=True)  7.41 us
    ppermute x4, starting transfers between devices, _resolve_series_all(): jax.lax.ppermute(taken_in, peer_axis, [(j0, j0 ^ y) for j0 in range(tall)])  6.92 us
    reshape x4, local copies, waits for them, and re-layouts, tile_update(): flat = outer.astype(jnp.bfloat16).reshape(count * columns, width * width)  6.79 us
    all_to_all x1, local copies, waits for them, and re-layouts, on_device(): lax.all_to_all(right, 'col', split_axis=1, concat_axis=0, tiled=True)  6.76 us
    dot_general x4, matrix products, tile_update(): jnp.einsum('sic,sje->ijce', left_rows, right_cols, preferred_element_type...  6.52 us
    dot_general x4, matrix products, tile_update(): jnp.dot(flat, out_weight, preferred_element_type=jnp.float32) + out_bias  6.39 us
  transfers between devices with their start and end apart: 6, of which 4 were waited for; matrix products, arithmetic and copies ran while one was open for 14% of the time, Pallas kernels for 0%

profile of v1, /device:TPU:0, one launch (start us, length us, event | category | flops | bytes accessed | tf_op | source)
XLA Modules:
  0.0 119.5 jit_solution(3331219254307533619)
XLA Ops:
  0.0 1.0 copy.24
  1.0 0.8 reshape.17
  1.7 7.4 %all-to-all-start = ((bf16[16,2,512]{2,1,0:T(2,128)(2,1)}), bf16[16,2,512]{2,1,0:T(2,128)(2,1)S(1)}, u32[]{:S(2)}, u32[]{:S(2)}) async-start(bf16[16,2,512]{2,1,0:T(2,128)(2,1)} %reshape.17), calls=%async_computation | async-start | bytes 65536 | tf_op jit(solution)/shard_map/all_to_all | solution.py:44
  9.1 6.9 %copy.19 = bf16[16,1280,32]{2,0,1:T(8,128)(2,1)} copy(bf16[16,1280,32]{1,2,0:T(8,128)(2,1)} %param.7) | data formatting | bytes 2621440 | tf_op args[1]
  16.0 8.3 %reshape.19 = bf16[16,2,20480]{2,1,0:T(2,128)(2,1)} reshape(bf16[1280,16,32]{2,1,0:T(8,128)(2,1)} %bitcast.49) | data formatting | bytes 2621440
  24.4 0.0 all-to-all-done
  24.4 6.0 %all-to-all-start.1 = ((bf16[16,2,20480]{2,1,0:T(2,128)(2,1)}), bf16[16,2,20480]{2,1,0:T(2,128)(2,1)S(1)}, u32[]{:S(2)}, u32[]{:S(2)}) async-start(bf16[16,2,20480]{2,1,0:T(2,128)(2,1)} %reshape.19), calls=%async_computation.1 | async-start | bytes 2621440 | tf_op jit(solution)/shard_map/all_to_all | solution.py:45
  30.4 0.1 reshape.18
  30.5 0.5 collective-permute-start
  31.0 0.1 copy.15
  31.1 0.9 collective-permute-done
  32.0 0.1 copy.16
  32.1 1.9 %collective-permute-start.1 = (bf16[256,4,32]{0,2,1:T(8,128)(2,1)S(1)}, bf16[256,4,32]{0,2,1:T(8,128)(2,1)S(1)}, u32[]{:S(2)}, u32[]{:S(2)}) collective-permute-start(bf16[256,4,32]{0,2,1:T(8,128)(2,1)S(1)} %maximum_select_fusion.3), channel_id=1, source_target_pairs={{0,2},{1,3},{2,0},{3,1},{4,6},{5,7},{6,4},{7,5},{8,10},{9,11},{10,... | collective-permute-start | bytes 196616 | tf_op jit(solution)/shard_map/ppermute | solution.py:12
  34.0 8.8 %collective-permute-done.1 = bf16[256,4,32]{0,2,1:T(8,128)(2,1)S(1)} collective-permute-done((bf16[256,4,32]{0,2,1:T(8,128)(2,1)S(1)}, bf16[256,4,32]{0,2,1:T(8,128)(2,1)S(1)}, u32[]{:S(2)}, u32[]{:S(2)}) %collective-permute-start.1) | collective-permute-done | bytes 65568 | tf_op jit(solution)/shard_map/ppermute | solution.py:12
  42.8 0.1 collective-permute-start.2
  42.9 12.6 %collective-permute-done.2 = bf16[256,8,32]{0,2,1:T(8,128)(2,1)S(1)} collective-permute-done((bf16[256,8,32]{0,2,1:T(8,128)(2,1)S(1)}, bf16[256,8,32]{0,2,1:T(8,128)(2,1)S(1)}, u32[]{:S(2)}, u32[]{:S(2)}) %collective-permute-start.2) | collective-permute-done | bytes 131104 | tf_op jit(solution)/shard_map/ppermute | solution.py:12
  55.5 4.4 %collective-permute-start.3 = (bf16[256,16,32]{0,2,1:T(8,128)(2,1)S(1)}, bf16[256,16,32]{0,2,1:T(8,128)(2,1)S(1)}, u32[]{:S(2)}, u32[]{:S(2)}) collective-permute-start(bf16[256,16,32]{0,2,1:T(8,128)(2,1)S(1)} %maximum_select_fusion.1), channel_id=1, source_target_pairs={{0,8},{1,9},{2,10},{3,11},{4,12},{5,13},{6,14},{7,15},{8,0},{9,1},... | collective-permute-start | bytes 786440 | tf_op jit(solution)/shard_map/ppermute | solution.py:12
  59.9 13.8 %collective-permute-done.3 = bf16[256,16,32]{0,2,1:T(8,128)(2,1)S(1)} collective-permute-done((bf16[256,16,32]{0,2,1:T(8,128)(2,1)S(1)}, bf16[256,16,32]{0,2,1:T(8,128)(2,1)S(1)}, u32[]{:S(2)}, u32[]{:S(2)}) %collective-permute-start.3) | collective-permute-done | bytes 262176 | tf_op jit(solution)/shard_map/ppermute | solution.py:12
  73.8 0.9 maximum_select_fusion
  74.7 4.0 %reshape.20 = bf16[1280,16,32]{2,1,0:T(8,128)(2,1)} reshape(bf16[16,2,20480]{2,1,0:T(2,128)(2,1)S(1)} %all-to-all-done.1) | data formatting | bytes 2621440
  78.7 6.8 %copy.20 = bf16[16,16,80,32]{2,3,0,1:T(8,128)(2,1)S(1)} copy(bf16[16,16,80,32]{3,0,2,1:T(8,128)(2,1)} %bitcast.48) | data formatting | bytes 2621440 | tf_op jit(solution)/shard_map/all_to_all | solution.py:45
  85.5 0.0 copy-start.2
  85.5 1.6 %copy.21 = bf16[256,80,32]{0,1,2:T(8,128)(2,1)S(1)} copy(bf16[256,80,32]{1,2,0:T(8,128)(2,1)S(1)} %bitcast.51) | data formatting | bytes 2621440 | tf_op jit(solution)/shard_map/while | solution.py:38
  87.1 32.4 %while.10 = (s32[]{:T(128)}, bf16[4,8,80,128]{3,2,1,0:T(8,128)(2,1)}, bf16[4,256,8,32]{1,3,2,0:T(8,128)(2,1)}, bf16[256,80,32]{0,1,2:T(8,128)(2,1)S(1)}, bf16[10...) while((s32[]{:T(128)}, bf16[4,8,80,128]{3,2,1,0:T(8,128)(2,1)}, bf16[4,256,8,32]{1,3,2,0:T(8,128)(2,1)}, ...), condition=%wide.region_1.2_spmd, body=%wide.region_0.1_spmd.sunk | while | flops 504791040 | bytes 20547204 | solution.py:38
  87.1 1.1 copy-done
  88.2 1.6 %fusion.18 = bf16[8,80,32,32]{1,2,3,0:T(8,128)(2,1)S(1)} fusion(bf16[256,80,32]{0,1,2:T(8,128)(2,1)S(1)} %get-tuple-element.116, bf16[4,256,8,32]{1,3,2,0:T(8,128)(2,1)} %get-tuple-element.115, s32[]{:T(128)} %get-tuple-element.106), kind=kOutput, calls=%fused_computation.1.clone.1 | convolution fusion | flops 336855040 | bytes 2753024 | tf_op jit(solution)/shard_map/while/body/eval_jaxpr/sic,sje->ijce/dot_general | solution.py:27
  89.8 1.4 %copy.26 = bf16[8,80,32,32]{1,0,3,2:T(8,128)(2,1)S(1)} copy(bf16[8,80,32,32]{1,2,3,0:T(8,128)(2,1)S(1)} %fusion.18) | data formatting | bytes 2621440 | tf_op jit(solution)/shard_map/while/body/eval_jaxpr/convert_element_type | solution.py:30
  91.2 1.7 %reshape.22 = bf16[640,1024]{0,1:T(8,128)(2,1)S(1)} reshape(bf16[8,80,32,32]{1,0,3,2:T(8,128)(2,1)S(1)} %copy.26) | data formatting | bytes 2621440 | tf_op jit(solution)/shard_map/while/body/eval_jaxpr/reshape | solution.py:30
  92.9 1.6 %fusion.19 = bf16[640,128]{1,0:T(8,128)(2,1)S(1)} fusion(bf16[640,1024]{0,1:T(8,128)(2,1)S(1)} %reshape.22, bf16[1024,128]{1,0:T(8,128)(2,1)} %get-tuple-element.117, f32[128]{0:T(128)S(1)} %get-tuple-element.118), kind=kOutput, calls=%fused_computation.4.clone.1 | convolution fusion | flops 167936000 | bytes 1737216 | tf_op jit(solution)/shard_map/while/body/eval_jaxpr/dot_general | solution.py:31
  94.5 0.7 constant_dynamic-update-slice_fusion.2
  95.2 1.1 copy-done
  96.3 1.6 %fusion.18 = bf16[8,80,32,32]{1,2,3,0:T(8,128)(2,1)S(1)} fusion(bf16[256,80,32]{0,1,2:T(8,128)(2,1)S(1)} %get-tuple-element.116, bf16[4,256,8,32]{1,3,2,0:T(8,128)(2,1)} %get-tuple-element.115, s32[]{:T(128)} %get-tuple-element.106), kind=kOutput, calls=%fused_computation.1.clone.1 | convolution fusion | flops 336855040 | bytes 2753024 | tf_op jit(solution)/shard_map/while/body/eval_jaxpr/sic,sje->ijce/dot_general | solution.py:27
  97.9 1.4 %copy.26 = bf16[8,80,32,32]{1,0,3,2:T(8,128)(2,1)S(1)} copy(bf16[8,80,32,32]{1,2,3,0:T(8,128)(2,1)S(1)} %fusion.18) | data formatting | bytes 2621440 | tf_op jit(solution)/shard_map/while/body/eval_jaxpr/convert_element_type | solution.py:30
  99.3 1.7 %reshape.22 = bf16[640,1024]{0,1:T(8,128)(2,1)S(1)} reshape(bf16[8,80,32,32]{1,0,3,2:T(8,128)(2,1)S(1)} %copy.26) | data formatting | bytes 2621440 | tf_op jit(solution)/shard_map/while/body/eval_jaxpr/reshape | solution.py:30
  101.0 1.6 %fusion.19 = bf16[640,128]{1,0:T(8,128)(2,1)S(1)} fusion(bf16[640,1024]{0,1:T(8,128)(2,1)S(1)} %reshape.22, bf16[1024,128]{1,0:T(8,128)(2,1)} %get-tuple-element.117, f32[128]{0:T(128)S(1)} %get-tuple-element.118), kind=kOutput, calls=%fused_computation.4.clone.1 | convolution fusion | flops 167936000 | bytes 1737216 | tf_op jit(solution)/shard_map/while/body/eval_jaxpr/dot_general | solution.py:31
  102.6 0.7 constant_dynamic-update-slice_fusion.2
  103.3 1.1 copy-done
  104.4 1.6 %fusion.18 = bf16[8,80,32,32]{1,2,3,0:T(8,128)(2,1)S(1)} fusion(bf16[256,80,32]{0,1,2:T(8,128)(2,1)S(1)} %get-tuple-element.116, bf16[4,256,8,32]{1,3,2,0:T(8,128)(2,1)} %get-tuple-element.115, s32[]{:T(128)} %get-tuple-element.106), kind=kOutput, calls=%fused_computation.1.clone.1 | convolution fusion | flops 336855040 | bytes 2753024 | tf_op jit(solution)/shard_map/while/body/eval_jaxpr/sic,sje->ijce/dot_general | solution.py:27
  106.0 1.4 %copy.26 = bf16[8,80,32,32]{1,0,3,2:T(8,128)(2,1)S(1)} copy(bf16[8,80,32,32]{1,2,3,0:T(8,128)(2,1)S(1)} %fusion.18) | data formatting | bytes 2621440 | tf_op jit(solution)/shard_map/while/body/eval_jaxpr/convert_element_type | solution.py:30
  107.4 1.7 %reshape.22 = bf16[640,1024]{0,1:T(8,128)(2,1)S(1)} reshape(bf16[8,80,32,32]{1,0,3,2:T(8,128)(2,1)S(1)} %copy.26) | data formatting | bytes 2621440 | tf_op jit(solution)/shard_map/while/body/eval_jaxpr/reshape | solution.py:30
  109.1 1.6 %fusion.19 = bf16[640,128]{1,0:T(8,128)(2,1)S(1)} fusion(bf16[640,1024]{0,1:T(8,128)(2,1)S(1)} %reshape.22, bf16[1024,128]{1,0:T(8,128)(2,1)} %get-tuple-element.117, f32[128]{0:T(128)S(1)} %get-tuple-element.118), kind=kOutput, calls=%fused_computation.4.clone.1 | convolution fusion | flops 167936000 | bytes 1737216 | tf_op jit(solution)/shard_map/while/body/eval_jaxpr/dot_general | solution.py:31
  110.7 0.7 constant_dynamic-update-slice_fusion.2
  111.4 1.1 copy-done
  112.5 1.6 %fusion.18 = bf16[8,80,32,32]{1,2,3,0:T(8,128)(2,1)S(1)} fusion(bf16[256,80,32]{0,1,2:T(8,128)(2,1)S(1)} %get-tuple-element.116, bf16[4,256,8,32]{1,3,2,0:T(8,128)(2,1)} %get-tuple-element.115, s32[]{:T(128)} %get-tuple-element.106), kind=kOutput, calls=%fused_computation.1.clone.1 | convolution fusion | flops 336855040 | bytes 2753024 | tf_op jit(solution)/shard_map/while/body/eval_jaxpr/sic,sje->ijce/dot_general | solution.py:27
  114.1 1.4 %copy.26 = bf16[8,80,32,32]{1,0,3,2:T(8,128)(2,1)S(1)} copy(bf16[8,80,32,32]{1,2,3,0:T(8,128)(2,1)S(1)} %fusion.18) | data formatting | bytes 2621440 | tf_op jit(solution)/shard_map/while/body/eval_jaxpr/convert_element_type | solution.py:30
  115.5 1.7 %reshape.22 = bf16[640,1024]{0,1:T(8,128)(2,1)S(1)} reshape(bf16[8,80,32,32]{1,0,3,2:T(8,128)(2,1)S(1)} %copy.26) | data formatting | bytes 2621440 | tf_op jit(solution)/shard_map/while/body/eval_jaxpr/reshape | solution.py:30
  117.2 1.6 %fusion.19 = bf16[640,128]{1,0:T(8,128)(2,1)S(1)} fusion(bf16[640,1024]{0,1:T(8,128)(2,1)S(1)} %reshape.22, bf16[1024,128]{1,0:T(8,128)(2,1)} %get-tuple-element.117, f32[128]{0:T(128)S(1)} %get-tuple-element.118), kind=kOutput, calls=%fused_computation.4.clone.1 | convolution fusion | flops 167936000 | bytes 1737216 | tf_op jit(solution)/shard_map/while/body/eval_jaxpr/dot_general | solution.py:31
  118.8 0.7 constant_dynamic-update-slice_fusion.2
  (19 shorter events, 0.1 us)
Async XLA Ops:
  1.7 22.6 %all-to-all-start = ((bf16[16,2,512]{2,1,0:T(2,128)(2,1)}), bf16[16,2,512]{2,1,0:T(2,128)(2,1)S(1)}, u32[]{:S(2)}, u32[]{:S(2)}) async-start(bf16[16,2,512]{2,1,0:T(2,128)(2,1)} %reshape.17), calls=%async_computation | async-start | bytes 65536 | tf_op jit(solution)/shard_map/all_to_all | solution.py:44
  24.4 50.3 %all-to-all-start.1 = ((bf16[16,2,20480]{2,1,0:T(2,128)(2,1)}), bf16[16,2,20480]{2,1,0:T(2,128)(2,1)S(1)}, u32[]{:S(2)}, u32[]{:S(2)}) async-start(bf16[16,2,20480]{2,1,0:T(2,128)(2,1)} %reshape.19), calls=%async_computation.1 | async-start | bytes 2621440 | tf_op jit(solution)/shard_map/all_to_all | solution.py:45
  30.5 1.5 %collective-permute-start = (bf16[256,2,32]{2,0,1:T(8,128)(2,1)S(1)}, bf16[256,2,32]{2,0,1:T(8,128)(2,1)S(1)}, u32[]{:S(2)}, u32[]{:S(2)}) collective-permute-start(bf16[256,2,32]{2,0,1:T(8,128)(2,1)S(1)} %bitcast.53), channel_id=1, source_target_pairs={{0,1},{1,0},{2,3},{3,2},{4,5},{5,4},{6,7},{7,6},{8,9},{9,8},{10,11... | collective-permute-start | bytes 98312 | tf_op jit(solution)/shard_map/ppermute | solution.py:12
  32.1 10.7 %collective-permute-start.1 = (bf16[256,4,32]{0,2,1:T(8,128)(2,1)S(1)}, bf16[256,4,32]{0,2,1:T(8,128)(2,1)S(1)}, u32[]{:S(2)}, u32[]{:S(2)}) collective-permute-start(bf16[256,4,32]{0,2,1:T(8,128)(2,1)S(1)} %maximum_select_fusion.3), channel_id=1, source_target_pairs={{0,2},{1,3},{2,0},{3,1},{4,6},{5,7},{6,4},{7,5},{8,10},{9,11},{10,... | collective-permute-start | bytes 196616 | tf_op jit(solution)/shard_map/ppermute | solution.py:12
  42.8 12.6 %collective-permute-start.2 = (bf16[256,8,32]{0,2,1:T(8,128)(2,1)S(1)}, bf16[256,8,32]{0,2,1:T(8,128)(2,1)S(1)}, u32[]{:S(2)}, u32[]{:S(2)}) collective-permute-start(bf16[256,8,32]{0,2,1:T(8,128)(2,1)S(1)} %maximum_select_fusion.2), channel_id=1, source_target_pairs={{0,4},{1,5},{2,6},{3,7},{4,0},{5,1},{6,2},{7,3},{8,12},{9,13},{10,... | collective-permute-start | bytes 393224 | tf_op jit(solution)/shard_map/ppermute | solution.py:12
  55.5 18.3 %collective-permute-start.3 = (bf16[256,16,32]{0,2,1:T(8,128)(2,1)S(1)}, bf16[256,16,32]{0,2,1:T(8,128)(2,1)S(1)}, u32[]{:S(2)}, u32[]{:S(2)}) collective-permute-start(bf16[256,16,32]{0,2,1:T(8,128)(2,1)S(1)} %maximum_select_fusion.1), channel_id=1, source_target_pairs={{0,8},{1,9},{2,10},{3,11},{4,12},{5,13},{6,14},{7,15},{8,0},{9,1},... | collective-permute-start | bytes 786440 | tf_op jit(solution)/shard_map/ppermute | solution.py:12
  85.5 1.6 %copy-start.2 = (f32[128]{0:T(128)S(1)}, f32[128]{0:T(128)}, u32[]{:S(2)}) copy-start(f32[128]{0:T(128)} %param.9) | copy-start | bytes 1540
  87.1 1.1 copy-start
  92.9 2.3 %copy-start.1 = (bf16[256,80,32]{0,1,2:T(8,128)(2,1)S(1)}, bf16[256,80,32]{0,1,2:T(8,128)(2,1)}, u32[]{:S(2)}) copy-start(bf16[256,80,32]{0,1,2:T(8,128)(2,1)} %copy-done) | copy-start | bytes 3932164 | tf_op jit(solution)/shard_map/while
  95.2 1.1 copy-start
  101.0 2.3 %copy-start.1 = (bf16[256,80,32]{0,1,2:T(8,128)(2,1)S(1)}, bf16[256,80,32]{0,1,2:T(8,128)(2,1)}, u32[]{:S(2)}) copy-start(bf16[256,80,32]{0,1,2:T(8,128)(2,1)} %copy-done) | copy-start | bytes 3932164 | tf_op jit(solution)/shard_map/while
  103.3 1.1 copy-start
  109.1 2.3 %copy-start.1 = (bf16[256,80,32]{0,1,2:T(8,128)(2,1)S(1)}, bf16[256,80,32]{0,1,2:T(8,128)(2,1)}, u32[]{:S(2)}) copy-start(bf16[256,80,32]{0,1,2:T(8,128)(2,1)} %copy-done) | copy-start | bytes 3932164 | tf_op jit(solution)/shard_map/while
  111.4 1.1 copy-start
  117.2 2.3 %copy-start.1 = (bf16[256,80,32]{0,1,2:T(8,128)(2,1)S(1)}, bf16[256,80,32]{0,1,2:T(8,128)(2,1)}, u32[]{:S(2)}) copy-start(bf16[256,80,32]{0,1,2:T(8,128)(2,1)} %copy-done) | copy-start | bytes 3932164 | tf_op jit(solution)/shard_map/while
